TPU v7x, 128 devices: a whole 4x4x4 slice. The times are simulated.
128 devices in a mesh: expert: 16 (over x_hi, y, core), row: 8 (over z, x_lo).
Axes of the slice: x: 4 (x_hi: 2, x_lo: 2; x = x_hi * 2 + x_lo), y: 4, z: 4, core: 2. Of those that a mesh axis runs over, the one named last changes fastest.
Arguments:
- weights: bfloat16 [16, 7168, 2048], P('expert', 'row'), may hold values from -6 to 6
- left_bits: int32 [16, 7168], P('expert', 'row'), may hold values from 0 to 1
- right_bits: int32 [16, 2048], P('expert'), may hold values from 0 to 1
- groups: int32 [16, 2048], P('expert'), may hold values from 0 to 15, never falling along the last dimension, each value on 1 to 256 neighbouring positions
Outputs:
- scaled: bfloat16 [16, 7168, 2048], P('expert', 'row')
- block_error: float32 [16, 7168, 256], P('expert', 'row')
- scales: float32 [16, 16], P('expert')
- expert_error: float32 [16], P('expert')
- total_error: float32 [], replicated
Inputs may be any that keep to these rules, and one draw needn't show every extreme that they name: Along each expert's 2048 columns the group number never falls; each of the 16 groups holds 1 to 256 columns.
All inputs are finite; a program needn't handle non-finite values.
Results may differ from a plain program's by a relative error of at most 0.0091.
Values may be sent and summed in bfloat16 or wider, within the bound.
A program may use at most 128 MiB of HBM per device.

v0:
```python
import math

import jax
import jax.numpy as jnp
from jax import lax
from jax.sharding import PartitionSpec as P

D = 7168
FF = 2048
HB = 128
OUTER = 16
GROUPS = 16
BLOCKS = 56


def from_everyone(value, axis):
    peers = lax.axis_size(axis)
    return lax.all_to_all(
        jnp.broadcast_to(value[None], (peers, *value.shape)), axis, 0, 0, tiled=True
    )


def over_copies(value, axis):
    everything = from_everyone(value, axis)
    return jnp.max(everything, axis=0)


def taken_together(value, axis):
    return from_everyone(value, axis).sum(axis=0)


def sylvester(order):
    row_index = jnp.arange(order, dtype=jnp.int32)[:, None]
    col_index = jnp.arange(order, dtype=jnp.int32)[None, :]
    common = jnp.bitwise_and(row_index, col_index)
    parity = jnp.zeros((order, order), jnp.int32)
    for bit_pos in range(order.bit_length() - 1):
        parity = parity + jnp.bitwise_and(jnp.right_shift(common, bit_pos), 1)
    return (1 - 2 * jnp.bitwise_and(parity, 1)).astype(jnp.float32)


def cosine_block(order):
    first = jnp.arange(order, dtype=jnp.float32)[:, None]
    second = jnp.arange(order, dtype=jnp.float32)[None, :]
    table = math.sqrt(2.0 / order) * jnp.cos(math.pi * (2.0 * second + 1.0) * first / (2.0 * order))
    return jnp.where(first == 0.0, table * math.sqrt(0.5), table)


def coset_error(values):
    nearest = jnp.floor(values + 0.5)
    offset = values - nearest
    squares = jnp.sum(offset * offset, axis=-1)
    largest = jnp.max(jnp.abs(offset), axis=-1)
    parity = jnp.mod(jnp.sum(nearest, axis=-1), 2.0)
    return jnp.where(parity > 0.5, squares + 1.0 - 2.0 * largest, squares)


def lattice_error(values):
    octets = values.reshape(values.shape[:-1] + (values.shape[-1] // 8, 8))
    return jnp.minimum(coset_error(octets), coset_error(octets - 0.5))


def row_transform(mixed_rows, row_hadamard):
    turned = jnp.einsum("eibf,bk->eikf", mixed_rows, row_hadamard, precision=lax.Precision.HIGHEST)
    return turned / math.sqrt(HB)


def weight_of_rows(first_row, count):
    positions = (first_row + jnp.arange(count, dtype=jnp.int32)).astype(jnp.float32)
    return (1.0 + 4.0 * (positions + 0.5) / D) / 3.0


def group_scale(rotated, group_cols):
    column_peak = jnp.max(jnp.abs(rotated), axis=1)
    group_ids = jnp.arange(GROUPS, dtype=jnp.int32)
    in_group = group_cols[:, None, :] == group_ids[None, :, None]
    partial_peak = jnp.max(jnp.where(in_group, column_peak[:, None, :], 0.0), axis=2)
    group_peak = jnp.maximum(over_copies(partial_peak, "row"), 1.0)
    column_scale = jnp.sum(jnp.where(in_group, (2.0 / group_peak)[:, :, None], 0.0), axis=1)
    return (group_peak, column_scale)


def body(weights, left_bits, right_bits, groups):
    experts, local_rows, width = weights.shape
    blocks_here = local_rows // HB
    column_hadamard = sylvester(width // OUTER).astype(jnp.bfloat16)
    outer_hadamard = sylvester(OUTER)
    row_hadamard = sylvester(HB)
    block_matrix = cosine_block(BLOCKS).astype(jnp.bfloat16)
    left_sign = (2 * left_bits - 1).astype(jnp.float32)
    right_sign = (2 * right_bits - 1).astype(jnp.float32)
    signed = (weights.astype(jnp.float32) * left_sign[:, :, None] * right_sign[:, None, :]).astype(
        jnp.bfloat16
    )
    shaped = signed.reshape(experts, local_rows, OUTER, width // OUTER)
    inner = jnp.einsum("erpq,qs->erps", shaped, column_hadamard, preferred_element_type=jnp.float32)
    outer = jnp.einsum("erps,pt->erts", inner, outer_hadamard, precision=lax.Precision.HIGHEST)
    columns = (outer.reshape(experts, local_rows, width) / math.sqrt(FF)).astype(jnp.bfloat16)
    blocked = columns.reshape(experts, blocks_here, HB, width)
    column_slab = lax.all_to_all(blocked, "row", split_axis=3, concat_axis=1, tiled=True)
    mixed_rows = jnp.einsum(
        "ij,ejbf->eibf", block_matrix, column_slab, preferred_element_type=jnp.float32
    )
    turned = row_transform(mixed_rows, row_hadamard)
    rotated = lax.all_to_all(
        turned.astype(jnp.bfloat16), "row", split_axis=1, concat_axis=3, tiled=True
    ).astype(turned.dtype)
    rotated = rotated.reshape(experts, local_rows, width)
    group_peak, column_scale = group_scale(rotated, groups)
    values = rotated * column_scale[:, None, :]
    block_errors = lattice_error(values)
    row_weight = weight_of_rows(lax.axis_index("row") * local_rows, local_rows)
    partial_error = jnp.sum(block_errors * row_weight[None, :, None], axis=(1, 2)) / (D * FF // 8)
    scaled = values.astype(jnp.bfloat16)
    expert_count = experts * lax.axis_size("expert")
    expert_error = taken_together(partial_error, "row")
    total_error = taken_together(jnp.sum(expert_error), "expert") / expert_count
    return (scaled, block_errors, group_peak / 2.0, expert_error, total_error)


def solution(mesh):
    placed = (P("expert", "row", None), P("expert", "row"), P("expert", None), P("expert", None))
    return jax.shard_map(
        body,
        mesh=mesh,
        in_specs=placed,
        out_specs=(
            P("expert", "row", None),
            P("expert", "row", None),
            P("expert", None),
            P("expert"),
            P(),
        ),
        check_vma=False,
    )
```

profile of v0, /device:TPU:0, one launch (start us, length us, event | category | flops | bytes accessed | tf_op | source)
XLA Modules:
  0.0 253.3 jit_solution(4140201884117918043)
XLA Ops:
  0.6 0.7 add_convert_fusion
  1.3 0.7 convert_reduce_fusion
  2.0 3.1 %fusion.4 = bf16[112,8,16,128]{3,1,2,0:T(8,128)(2,1)S(1)} fusion(bf16[1,896,2048]{2,1,0:T(8,128)(2,1)} %param.4, f32[2048]{0:T(1024)S(1)} %bitcast.116, f32[896]{0:T(1024)S(1)} %convert_reduce_fusion), kind=kLoop, calls=%fused_computation.16 | loop fusion | flops 7340032 | bytes 7351808
  5.1 1.2 copy.61
  6.3 1.1 fusion.24
  7.5 8.3 %fusion.5 = bf16[1,896,16,128]{3,2,1,0:T(8,128)(2,1)} fusion(f32[896,16,128]{2,1,0:T(8,128)S(1)} %fusion.24), kind=kOutput, calls=%fused_computation.17 | convolution fusion | flops 355995648 | bytes 11010048 | tf_op jit(solution)/shard_map/erps,pt->erts/dot_general | solution.py:97
  15.8 6.7 %convert_element_type.172 = bf16[1,7,128,2048]{3,2,1,0:T(8,128)(2,1)} reshape(bf16[1,896,16,128]{3,2,1,0:T(8,128)(2,1)} %fusion.5) | data formatting | bytes 7340032 | tf_op jit(solution)/shard_map/convert_element_type | solution.py:98
  22.5 6.5 %copy.44 = bf16[1,7,128,2048]{2,1,0,3:T(8,128)(2,1)} copy(bf16[1,7,128,2048]{3,2,1,0:T(8,128)(2,1)} %convert_element_type.172) | data formatting | bytes 7340032 | tf_op jit(solution)/shard_map/convert_element_type | solution.py:98
  29.0 6.4 %all-to-all-start = ((bf16[1,7,128,2048]{2,1,0,3:T(8,128)(2,1)}), bf16[1,7,128,2048]{2,1,0,3:T(8,128)(2,1)}, u32[]{:S(2)}, u32[]{:S(2)}) async-start(bf16[1,7,128,2048]{2,1,0,3:T(8,128)(2,1)} %copy.44), calls=%async_computation | async-start | bytes 8388608 | tf_op jit(solution)/shard_map/all_to_all | solution.py:100
  35.4 49.5 %all-to-all-done = bf16[1,7,128,2048]{2,1,0,3:T(8,128)(2,1)} async-done(((bf16[1,7,128,2048]{2,1,0,3:T(8,128)(2,1)}), bf16[1,7,128,2048]{2,1,0,3:T(8,128)(2,1)}, u32[]{:S(2)}, u32[]{:S(2)}) %all-to-all-start) | async-done | bytes 3670048 | tf_op jit(solution)/shard_map/all_to_all | solution.py:100
  84.9 4.5 %copy.45 = bf16[1,7,128,2048]{2,3,1,0:T(8,128)(2,1)} copy(bf16[1,7,128,2048]{2,1,0,3:T(8,128)(2,1)} %all-to-all-done) | data formatting | bytes 7340032 | tf_op jit(solution)/shard_map/all_to_all | solution.py:100
  89.4 6.3 %copy.46 = bf16[1,8,7,128,256]{4,3,2,1,0:T(8,128)(2,1)} copy(bf16[1,8,7,128,256]{3,4,1,2,0:T(8,128)(2,1)} %bitcast.110) | data formatting | bytes 7340032 | tf_op jit(solution)/shard_map/all_to_all | solution.py:100
  95.7 5.1 %fusion.9 = f32[56,128,256]{2,0,1:T(8,128)S(1)} fusion(bf16[56,128,256]{2,1,0:T(8,128)(2,1)} %bitcast.109, f32[56]{0:T(128)S(1)} %add_multiply_fusion.1, pred[56]{0:T(512)(128)(4,1)S(1)} %iota_compare_fusion.1), kind=kOutput, calls=%fused_computation.21 | convolution fusion | flops 205539712 | bytes 11010328 | tf_op jit(solution)/shard_map/ij,ejbf->eibf/dot_general | solution.py:101
  100.8 9.8 %fusion.6 = bf16[1,56,128,256]{3,2,0,1:T(8,128)(2,1)} fusion(f32[56,128,256]{2,0,1:T(8,128)S(1)} %fusion.9), kind=kOutput, calls=%fused_computation.18 | convolution fusion | flops 2822651904 | bytes 11010048 | tf_op jit(solution)/shard_map/eibf,bk->eikf/dot_general | solution.py:64
  110.6 0.0 copy-start
  110.6 4.7 %all-to-all-start.1 = ((bf16[1,56,128,256]{3,2,0,1:T(8,128)(2,1)}), bf16[1,56,128,256]{3,2,0,1:T(8,128)(2,1)}, u32[]{:S(2)}, u32[]{:S(2)}) async-start(bf16[1,56,128,256]{3,2,0,1:T(8,128)(2,1)} %fusion.6), calls=%async_computation.1 | async-start | bytes 7340032 | tf_op jit(solution)/shard_map/all_to_all | solution.py:105
  115.3 43.0 %all-to-all-done.1 = bf16[1,56,128,256]{3,2,0,1:T(8,128)(2,1)} async-done(((bf16[1,56,128,256]{3,2,0,1:T(8,128)(2,1)}), bf16[1,56,128,256]{3,2,0,1:T(8,128)(2,1)}, u32[]{:S(2)}, u32[]{:S(2)}) %all-to-all-start.1) | async-done | bytes 3670048 | tf_op jit(solution)/shard_map/all_to_all | solution.py:105
  158.3 3.2 %abs_reduce_fusion.2 = f32[56,256]{1,0:T(8,128)S(1)} fusion(bf16[1,56,128,256]{3,2,0,1:T(8,128)(2,1)} %all-to-all-done.1), kind=kLoop, calls=%fused_computation.11 | loop fusion | flops 5490688 | bytes 3727360 | tf_op jit(solution)/shard_map/reduce_max | solution.py:74
  161.5 0.0 copy-done
  161.5 0.1 select_reduce_fusion.1
  161.7 0.6 broadcast_in_dim.42
  162.3 3.5 %all-to-all-start.2 = ((f32[8,1,16]{2,1,0:T(1,128)}), f32[8,1,16]{2,1,0:T(1,128)S(1)}, u32[]{:S(2)}, u32[]{:S(2)}) async-start(f32[8,1,16]{2,1,0:T(1,128)} %broadcast_in_dim.42), calls=%async_computation.2 | async-start | bytes 8192 | tf_op jit(solution)/shard_map/all_to_all | solution.py:18
  165.8 7.0 %copy.50 = f32[1,8,7,128,256]{3,2,4,1,0:T(8,128)} copy(bf16[1,8,7,128,256]{4,3,2,1,0:T(8,128)(2,1)} %bitcast.95) | data formatting | bytes 11010048 | tf_op jit(solution)/shard_map/convert_element_type | solution.py:107
  172.8 9.2 %reshape.657 = f32[1,896,256,8]{1,3,2,0:T(8,128)} reshape(f32[1,7,128,8,256]{2,1,4,3,0:T(8,128)} %bitcast.107) | data formatting | bytes 14680064 | tf_op jit(solution)/shard_map/convert_element_type | solution.py:107
  182.1 9.3 %reshape.664 = f32[1,896,2048]{1,2,0:T(8,128)} reshape(f32[1,7,128,8,256]{2,1,4,3,0:T(8,128)} %bitcast.108) | data formatting | bytes 14680064 | tf_op jit(solution)/shard_map/convert_element_type | solution.py:107
  191.3 8.6 %copy.58 = f32[1,896,2048]{2,1,0:T(8,128)} copy(f32[1,896,2048]{1,2,0:T(8,128)} %reshape.664) | data formatting | bytes 14680064 | tf_op jit(solution)/shard_map/convert_element_type | solution.py:107
  199.9 0.0 all-to-all-done.2
  200.0 0.5 multiply_bitcast_fusion
  200.5 0.1 select_reduce_fusion
  200.6 0.1 mul.272
  200.7 19.5 %fusion.3 = (f32[896,256]{0,1:T(8,128)S(1)}, f32[896,256]{0,1:T(8,128)S(1)}, f32[896,256]{0,1:T(8,128)S(1)}, f32[896,256]{0,1:T(8,128)S(1)}, f32[896,256]{0,1:T(8,128)S(1)}, /*index=5*/f32[896,256]{0,1:T(8,128)S(1)}) fusion(f32[1,896,256,8]{1,3,2,0:T(8,128)} %reshape.657, f32[256,8]{1,0:T(8,128)S(1)} %mul.272), kind=kLoop, calls=%fused_computation.9 | loop fusion | flops 29818880 | bytes 12853248 | tf_op jit(solution)/shard_map/reduce_sum | solution.py:54
  220.2 1.9 multiply_reduce_fusion.2
  222.7 0.6 broadcast_in_dim.44
  223.3 5.4 %all-to-all-start.3 = ((f32[8,1,1]{2,1,0:T(1,128)}), f32[8,1,1]{2,1,0:T(1,128)S(1)}, u32[]{:S(2)}, u32[]{:S(2)}) async-start(f32[8,1,1]{2,1,0:T(1,128)} %broadcast_in_dim.44), calls=%async_computation.3 | async-start | bytes 8192 | tf_op jit(solution)/shard_map/all_to_all | solution.py:18
  228.7 5.9 %multiply_convert_fusion = bf16[1,896,2048]{2,1,0:T(8,128)(2,1)} fusion(f32[1,896,2048]{2,1,0:T(8,128)} %copy.58, f32[2048]{0:T(1024)S(1)} %select_reduce_fusion), kind=kLoop, calls=%fused_computation.10 | loop fusion | flops 3670016 | bytes 11018240 | tf_op jit(solution)/shard_map/convert_element_type | solution.py:114
  234.7 0.2 all-to-all-done.3
  234.8 0.6 reduce_sum.90
  235.5 1.2 broadcast_in_dim.45
  236.7 6.7 %all-to-all-start.4 = ((f32[16,1,1]{2,1,0:T(1,128)}), f32[16,1,1]{2,1,0:T(1,128)S(1)}, u32[]{:S(2)}, u32[]{:S(2)}) async-start(f32[16,1,1]{2,1,0:T(1,128)} %broadcast_in_dim.45), calls=%async_computation.4 | async-start | bytes 16384 | tf_op jit(solution)/shard_map/all_to_all | solution.py:18
  243.4 1.2 copy.55
  244.7 6.2 %all-to-all-done.4 = f32[16,1,1]{2,1,0:T(1,128)S(1)} async-done(((f32[16,1,1]{2,1,0:T(1,128)}), f32[16,1,1]{2,1,0:T(1,128)S(1)}, u32[]{:S(2)}, u32[]{:S(2)}) %all-to-all-start.4) | async-done | bytes 96 | tf_op jit(solution)/shard_map/all_to_all | solution.py:18
  250.9 0.6 reduce_sum.92
  (7 shorter events, 0.1 us)
Async XLA Ops:
  29.0 55.9 %all-to-all-start = ((bf16[1,7,128,2048]{2,1,0,3:T(8,128)(2,1)}), bf16[1,7,128,2048]{2,1,0,3:T(8,128)(2,1)}, u32[]{:S(2)}, u32[]{:S(2)}) async-start(bf16[1,7,128,2048]{2,1,0,3:T(8,128)(2,1)} %copy.44), calls=%async_computation | async-start | bytes 8388608 | tf_op jit(solution)/shard_map/all_to_all | solution.py:100
  110.6 50.9 %copy-start = (s32[1,2048]{1,0:T(1,128)S(1)}, s32[1,2048]{1,0:T(1,128)}, u32[]{:S(2)}) copy-start(s32[1,2048]{1,0:T(1,128)} %param.7) | copy-start | bytes 24580
  110.6 47.7 %all-to-all-start.1 = ((bf16[1,56,128,256]{3,2,0,1:T(8,128)(2,1)}), bf16[1,56,128,256]{3,2,0,1:T(8,128)(2,1)}, u32[]{:S(2)}, u32[]{:S(2)}) async-start(bf16[1,56,128,256]{3,2,0,1:T(8,128)(2,1)} %fusion.6), calls=%async_computation.1 | async-start | bytes 7340032 | tf_op jit(solution)/shard_map/all_to_all | solution.py:105
  162.3 37.7 %all-to-all-start.2 = ((f32[8,1,16]{2,1,0:T(1,128)}), f32[8,1,16]{2,1,0:T(1,128)S(1)}, u32[]{:S(2)}, u32[]{:S(2)}) async-start(f32[8,1,16]{2,1,0:T(1,128)} %broadcast_in_dim.42), calls=%async_computation.2 | async-start | bytes 8192 | tf_op jit(solution)/shard_map/all_to_all | solution.py:18
  223.3 11.5 %all-to-all-start.3 = ((f32[8,1,1]{2,1,0:T(1,128)}), f32[8,1,1]{2,1,0:T(1,128)S(1)}, u32[]{:S(2)}, u32[]{:S(2)}) async-start(f32[8,1,1]{2,1,0:T(1,128)} %broadcast_in_dim.44), calls=%async_computation.3 | async-start | bytes 8192 | tf_op jit(solution)/shard_map/all_to_all | solution.py:18
  236.7 14.2 %all-to-all-start.4 = ((f32[16,1,1]{2,1,0:T(1,128)}), f32[16,1,1]{2,1,0:T(1,128)S(1)}, u32[]{:S(2)}, u32[]{:S(2)}) async-start(f32[16,1,1]{2,1,0:T(1,128)} %broadcast_in_dim.45), calls=%async_computation.4 | async-start | bytes 16384 | tf_op jit(solution)/shard_map/all_to_all | solution.py:18
where the time goes:
time: 256 us; the launch traced here: 253 us
  waiting for transfers between devices  98.9 us (39%)
  local copies, waits for them, and re-layouts  63.1 us (25%)
  other arithmetic  37 us (14%)
  starting transfers between devices  26.7 us (10%)
  matrix products  24.4 us (10%)
  between operations  3.19 us (1%)
    all_to_all x1, waiting for transfers between devices, body(): lax.all_to_all(blocked, 'row', split_axis=3, concat_axis=1, tiled=True)  49.5 us
    all_to_all x1, waiting for transfers between devices, body(): lax.all_to_all(turned.astype(jnp.bfloat16), 'row', split_axis=1, concat_a...  43 us
    convert_element_type x4, local copies, waits for them, and re-layouts, body(): rotated = lax.all_to_all(turned.astype(jnp.bfloat16), 'row', split_axis=1...  34.1 us
    reduce_sum x1, other arithmetic, coset_error(): parity = jnp.mod(jnp.sum(nearest, axis=-1), 2.0)  19.5 us
    all_to_all x3, starting transfers between devices, from_everyone(): lax.all_to_all(jnp.broadcast_to(value[None], (peers, *value.shape)), axis...  15.7 us
    convert_element_type x2, local copies, waits for them, and re-layouts, body(): (outer.reshape(experts, local_rows, width) / math.sqrt(FF)).astype(jnp.bf...  13.1 us
    all_to_all x2, local copies, waits for them, and re-layouts, body(): lax.all_to_all(blocked, 'row', split_axis=3, concat_axis=1, tiled=True)  10.8 us
    dot_general x1, matrix products, row_transform(): jnp.einsum('eibf,bk->eikf', mixed_rows, row_hadamard, precision=lax.Preci...  9.8 us
  transfers between devices with their start and end apart: 5, of which 4 were waited for; matrix products, arithmetic and copies ran while one was open for 16% of the time, Pallas kernels for 0%

commit v1 on v0

v1 whole, which is shorter than its diff:
```python
import functools
import math

import jax
import jax.numpy as jnp
import ml_dtypes
import numpy as np
from jax import lax
from jax.experimental import pallas as pl
from jax.experimental.pallas import tpu as pltpu
from jax.sharding import PartitionSpec as P

D = 7168
FF = 2048
HB = 128
GROUPS = 16
BLOCKS = 56
ROWS = 8
PEERS = 16
MINE = BLOCKS // ROWS
LANES = 128
MESH = pl.DeviceIdType.MESH
F32 = jnp.float32
BF16 = jnp.bfloat16


def cosine_table():
    first = np.arange(BLOCKS, dtype=np.float64)[:, None]
    second = np.arange(BLOCKS, dtype=np.float64)[None, :]
    table = math.sqrt(2.0 / BLOCKS) * np.cos(math.pi * (2.0 * second + 1.0) * first / (2.0 * BLOCKS))
    table[0] *= math.sqrt(0.5)
    padded = np.zeros((64, LANES), np.float32)
    padded[:BLOCKS, :BLOCKS] = table
    return padded.astype(ml_dtypes.bfloat16)


def iota(shape, dim):
    return lax.broadcasted_iota(jnp.int32, shape, dim)


def sign_of(common, bits):
    parity = common
    shift = bits // 2
    while shift:
        parity = jnp.bitwise_xor(parity, jnp.right_shift(parity, shift))
        shift //= 2
    return (1 - 2 * jnp.bitwise_and(parity, 1)).astype(F32)


def butterfly(parts):
    parts = list(parts)
    step = 1
    while step < len(parts):
        for low in range(len(parts)):
            if not low & step:
                a, b = parts[low], parts[low + step]
                parts[low], parts[low + step] = a + b, a - b
        step *= 2
    return parts


def odd(count):
    return count - 2.0 * jnp.floor(count * 0.5) > 0.5


def lattice(values):
    first = None
    for value in values:
        whole = jnp.floor(value)
        g = jnp.abs((value - whole) - 0.5)
        near = jnp.floor(value + 0.5)
        now = (g, g * g, g, g, whole, near)
        if first is None:
            first = now
        else:
            first = (
                first[0] + now[0],
                first[1] + now[1],
                jnp.maximum(first[2], g),
                jnp.minimum(first[3], g),
                first[4] + whole,
                first[5] + near,
            )
    total, squares, most, least, halves, wholes = first
    shifted = jnp.where(odd(halves), squares + 1.0 - 2.0 * most, squares)
    plain = 2.0 - total + squares
    plain = jnp.where(odd(wholes), plain + 2.0 * least, plain)
    return jnp.minimum(plain, shifted)


def kernel(
    w_ref, lb_ref, rb_ref, g_ref, cos_ref,
    scaled_ref, err_ref, scale_ref, expert_ref, total_ref,
    wv, had, perm, mix, right, left, signed, inner, sb1, rb1, mid, rot, rb2, ybuf,
    gperm, cs_nat, cs_perm, pk_s, pk_r, e_s, e_r, t_s, t_r,
    w_sem, s1_send, s1_recv, s2_send, s2_recv, pk_send, pk_recv, e_send, e_recv, t_send, t_recv,
):
    me = lax.axis_index("row")
    ex = lax.axis_index("expert")
    row_peer = [lax.rem(me + k, ROWS) for k in range(1, ROWS)]
    ex_peer = [lax.rem(ex + k, PEERS) for k in range(1, PEERS)]

    loads = []
    for i in range(MINE):
        loads.append(pltpu.make_async_copy(w_ref.at[0, pl.ds(i * HB, HB)], wv.at[pl.ds(i * HB, HB)], w_sem.at[i]))
        loads[-1].start()
    barrier = pltpu.get_barrier_semaphore()
    for p in row_peer:
        pl.semaphore_signal(barrier, inc=1, device_id={"row": p}, device_id_type=MESH)
    for p in ex_peer:
        pl.semaphore_signal(barrier, inc=1, device_id={"expert": p}, device_id_type=MESH)

    had[...] = sign_of(jnp.bitwise_and(iota((256, 256), 0), iota((256, 256), 1)), 8).astype(BF16)
    right[...] = jnp.broadcast_to((2 * rb_ref[...] - 1).astype(F32), (16, FF)).astype(BF16)
    for i in range(MINE):
        signs = (2 * lb_ref[:, i * HB:(i + 1) * HB] - 1).astype(F32)
        left[i] = jnp.broadcast_to(signs, (HB, LANES)).T.astype(BF16)

    for load in loads:
        load.wait()

    def column_block(i, carry):
        first = pl.multiple_of(i * HB, HB)
        lefts = jnp.concatenate([left[i], left[i]], axis=1)
        for p in range(8):
            x = wv[pl.ds(first, HB), p * 256:(p + 1) * 256]
            signed[p * HB:(p + 1) * HB, :] = x * lefts * right[0:1, p * 256:(p + 1) * 256]
        inner[...] = jnp.dot(signed[...], had[...], preferred_element_type=F32)
        for u in range(2):
            for r in range(HB // 16):
                parts = [inner[p * HB + r * 16:p * HB + (r + 1) * 16, u * LANES:(u + 1) * LANES] for p in range(8)]
                for t, part in enumerate(butterfly(parts)):
                    sb1[t // 4, (t % 4) * 2 + u, i, r * 16:(r + 1) * 16, :] = (part * (1.0 / math.sqrt(FF))).astype(BF16)
        return carry

    lax.fori_loop(0, MINE, column_block, 0)
    pl.semaphore_wait(barrier, ROWS + PEERS - 2)

    for h in range(2):
        for p in row_peer:
            pltpu.make_async_remote_copy(
                sb1.at[h, p], rb1.at[h, me], s1_send.at[h], s1_recv.at[h], device_id={"row": p}, device_id_type=MESH
            ).start()
    for h in range(2):
        rb1[h, me] = sb1[h, me]

    pick_a = (jnp.right_shift(iota((896, 64), 0), 4) == iota((896, 64), 1)).astype(F32).astype(BF16)
    spread = jnp.dot(pick_a, cos_ref[...], preferred_element_type=F32).astype(BF16)
    pick_j = (jnp.right_shift(iota((LANES, 896), 1), 4) == iota((LANES, 896), 0)).astype(F32).astype(BF16)
    mix[...] = jnp.dot(spread, pick_j, preferred_element_type=F32).astype(BF16)
    small = sign_of(
        jnp.bitwise_and(jnp.bitwise_and(iota((16, 896), 0), iota((16, 896), 1)), 15), 4
    ).astype(BF16)

    def sign_mix(a, carry):
        at = pl.ds(pl.multiple_of(a * 16, 16), 16)
        mix[at, :] = mix[at, :] * small
        return carry

    lax.fori_loop(0, BLOCKS, sign_mix, 0)
    for s in range(8):
        perm[:, s * LANES:(s + 1) * LANES] = (
            iota((1024, LANES), 0) == 8 * iota((1024, LANES), 1) + s
        ).astype(F32).astype(BF16)
    which = iota((16, 1024), 0)
    ids = jnp.zeros((16, 1024), F32)
    for h in range(2):
        ids = jnp.where(which == h, g_ref[:, h * 1024:(h + 1) * 1024].astype(F32), ids)
        own = g_ref[:, pl.ds(pl.multiple_of(h * 1024 + me * LANES, LANES), LANES)].astype(F32)
        ids = jnp.where(which == 2 + h, jnp.concatenate([own] * 8, axis=1), ids)
    gperm[...] = jnp.dot(ids.astype(BF16), perm[...], preferred_element_type=F32)

    def rotate_rows(h):
        pltpu.make_async_copy(rb1.at[h, pl.ds(0, ROWS - 1)], rb1.at[h, pl.ds(0, ROWS - 1)], s1_recv.at[h]).wait()

        def mix_blocks(q, carry):
            parts = []
            for half in range(2):
                at = pl.ds(pl.multiple_of(q * 32 + half * 16, 16), 16)
                parts.append(rb1[h, :, :, at, :].reshape(896, LANES))
            out = jnp.dot(mix[...], jnp.concatenate(parts, axis=1), preferred_element_type=F32)
            mid[2 * q] = out[:, :LANES]
            mid[2 * q + 1] = out[:, LANES:]
            return carry

        lax.fori_loop(0, 4, mix_blocks, 0)

        def turn(a, peak):
            at = pl.ds(pl.multiple_of(a * 16, 16), 16)
            parts = butterfly([mid[q, at, :] for q in range(8)])
            for q, part in enumerate(parts):
                part = part * (1.0 / math.sqrt(HB))
                peak = jnp.maximum(peak, jnp.abs(part))
                rot[h, a // MINE, lax.rem(a, MINE), q * 16:(q + 1) * 16, :] = part.astype(BF16)
            return peak

        peak = lax.fori_loop(0, BLOCKS, turn, jnp.zeros((16, LANES), F32))
        rb2[h, me] = rot[h, me]
        return jnp.max(peak, axis=0, keepdims=True)

    def send_rows(h, blocks):
        for i in blocks:
            for p in row_peer:
                pltpu.make_async_remote_copy(
                    rot.at[h, p, i], rb2.at[h, me, i], s2_send.at[h], s2_recv.at[h, i], device_id={"row": p}, device_id_type=MESH
                ).start()

    def exchange(slots, own, source, send, recv, here, peers, axis):
        slots[here] = own
        source[...] = own
        for p in peers:
            pltpu.make_async_remote_copy(
                source, slots.at[here], send, recv, device_id={axis: p}, device_id_type=MESH
            ).start()

    def arrived(slots, recv, count):
        pltpu.make_async_copy(slots.at[pl.ds(0, count)], slots.at[pl.ds(0, count)], recv).wait()

    col_peak = [rotate_rows(0)]
    send_rows(0, range(0, 2))
    col_peak.append(rotate_rows(1))

    group_id = iota((GROUPS, LANES), 0)
    most = jnp.zeros((GROUPS, LANES), F32)
    for h in range(2):
        own = g_ref[:, pl.ds(pl.multiple_of(h * 1024 + me * LANES, LANES), LANES)]
        most = jnp.maximum(most, jnp.where(group_id == own, col_peak[h], 0.0))
    most = jnp.broadcast_to(jnp.max(most, axis=1, keepdims=True), (GROUPS, LANES))
    exchange(pk_r, most, pk_s, pk_send, pk_recv, me, row_peer, "row")
    send_rows(0, range(2, MINE))

    arrived(pk_r, pk_recv, ROWS - 1)
    group_peak = jnp.ones((GROUPS, LANES), F32)
    for k in range(ROWS):
        group_peak = jnp.maximum(group_peak, pk_r[k])
    scale_row = jnp.sum(
        jnp.where(group_id == iota((GROUPS, LANES), 1), group_peak * 0.5, 0.0), axis=0, keepdims=True
    )
    scale_ref[...] = scale_row[:, :GROUPS]
    inverse = 2.0 / group_peak
    for m in range(16):
        ids = g_ref[:, m * LANES:(m + 1) * LANES]
        cs_nat[m:m + 1, :] = jnp.sum(jnp.where(group_id == ids, inverse, 0.0), axis=0, keepdims=True)
    for k in range(4):
        for s in range(8):
            ids = gperm[k:k + 1, s * LANES:(s + 1) * LANES]
            cs_perm[k, s:s + 1, :] = jnp.sum(
                jnp.where(group_id.astype(F32) == ids, inverse, 0.0), axis=0, keepdims=True
            )

    def own_errors(n, total):
        parts = []
        for h in range(2):
            blocks = []
            for k in range(8):
                a = n * 8 + k
                blocks.append(rot[h, a // MINE, lax.rem(a, MINE)])
            parts.append(jnp.concatenate(blocks, axis=1))
        ybuf[...] = jnp.dot(jnp.concatenate(parts, axis=0), perm[...], preferred_element_type=F32)
        block = n * 8 + jnp.right_shift(iota((8, LANES), 1), 4)
        for h in range(2):
            scales = [cs_perm[2 + h, s:s + 1, :] for s in range(8)]

            def rows(r, total):
                at = pl.ds(pl.multiple_of(h * HB + r * 8, 8), 8)
                errors = lattice([ybuf[at, s * LANES:(s + 1) * LANES] * scales[s] for s in range(8)])
                row = (block * HB + r * 8 + iota((8, LANES), 0)).astype(F32)
                return total + errors * ((1.0 + 4.0 * (row + 0.5) / D) / 3.0)

            total = lax.fori_loop(0, HB // 8, rows, total, unroll=4)
        return total

    error = lax.fori_loop(0, MINE, own_errors, jnp.zeros((8, LANES), F32))
    exchange(e_r, error, e_s, e_send, e_recv, me, row_peer, "row")
    send_rows(1, range(0, 2))

    def finish(h, i):
        pltpu.make_async_copy(
            rb2.at[h, pl.ds(0, ROWS - 1), i], rb2.at[h, pl.ds(0, ROWS - 1), i], s2_recv.at[h, i]
        ).wait()
        first = pl.multiple_of(i * HB, HB)
        blocks = [rb2[h, k, i] for k in range(ROWS)]
        ybuf[:HB, :] = jnp.dot(jnp.concatenate(blocks, axis=1), perm[...], preferred_element_type=F32)
        for k in range(ROWS):
            m = h * 8 + k
            scaled_ref[0, pl.ds(first, HB), m * LANES:(m + 1) * LANES] = (
                blocks[k].astype(F32) * cs_nat[m:m + 1, :]
            ).astype(BF16)
        scales = [cs_perm[h, s:s + 1, :] for s in range(8)]

        def rows(r, carry):
            at = pl.ds(pl.multiple_of(r * 8, 8), 8)
            errors = lattice([ybuf[at, s * LANES:(s + 1) * LANES] * scales[s] for s in range(8)])
            err_ref[0, pl.ds(pl.multiple_of(first + r * 8, 8), 8), h * LANES:(h + 1) * LANES] = errors
            return carry

        lax.fori_loop(0, HB // 8, rows, 0, unroll=4)

    def finish_many(h, start, stop):
        def step(i, carry):
            finish(h, i)
            return carry

        lax.fori_loop(start, stop, step, 0)

    finish_many(0, 0, 3)
    arrived(e_r, e_recv, ROWS - 1)
    error = e_r[0]
    for k in range(1, ROWS):
        error = error + e_r[k]
    error = jnp.sum(jnp.sum(error, axis=1, keepdims=True), axis=0, keepdims=True) * (1.0 / (D * FF // 8))
    expert_ref[...] = error
    exchange(t_r, jnp.broadcast_to(error, (8, LANES)), t_s, t_send, t_recv, ex, ex_peer, "expert")
    send_rows(1, range(2, MINE))
    finish_many(0, 3, MINE)
    arrived(t_r, t_recv, PEERS - 1)
    total = t_r[0]
    for k in range(1, PEERS):
        total = total + t_r[k]
    total_ref[...] = total[:1, :1] * (1.0 / PEERS)
    finish_many(1, 0, MINE)

    for h in range(2):
        pltpu.make_async_copy(sb1.at[h, pl.ds(0, ROWS - 1)], sb1.at[h, pl.ds(0, ROWS - 1)], s1_send.at[h]).wait()
        pltpu.make_async_copy(rot.at[h, pl.ds(0, ROWS - 1)], rot.at[h, pl.ds(0, ROWS - 1)], s2_send.at[h]).wait()
    arrived(pk_r, pk_send, ROWS - 1)
    arrived(e_r, e_send, ROWS - 1)
    arrived(t_r, t_send, PEERS - 1)


def body(weights, left_bits, right_bits, groups):
    vmem = pl.BlockSpec(memory_space=pltpu.VMEM)
    any_space = pl.BlockSpec(memory_space=pl.ANY)
    scaled, errors, scales, expert_error, total_error = pl.pallas_call(
        kernel,
        out_shape=(
            jax.ShapeDtypeStruct((1, MINE * HB, FF), BF16),
            jax.ShapeDtypeStruct((1, MINE * HB, FF // 8), F32),
            jax.ShapeDtypeStruct((1, GROUPS), F32),
            jax.ShapeDtypeStruct((1, 1), F32),
            jax.ShapeDtypeStruct((1, 1), F32),
        ),
        in_specs=[any_space, vmem, vmem, vmem, vmem],
        out_specs=(vmem,) * 5,
        scratch_shapes=[
            pltpu.VMEM((MINE * HB, FF), BF16),
            pltpu.VMEM((256, 256), BF16),
            pltpu.VMEM((1024, 1024), BF16),
            pltpu.VMEM((896, 896), BF16),
            pltpu.VMEM((16, FF), BF16),
            pltpu.VMEM((MINE, HB, LANES), BF16),
            pltpu.VMEM((8 * HB, 256), BF16),
            pltpu.VMEM((8 * HB, 256), F32),
            pltpu.VMEM((2, ROWS, MINE, HB, LANES), BF16),
            pltpu.VMEM((2, ROWS, MINE, HB, LANES), BF16),
            pltpu.VMEM((8, 896, LANES), F32),
            pltpu.VMEM((2, ROWS, MINE, HB, LANES), BF16),
            pltpu.VMEM((2, ROWS, MINE, HB, LANES), BF16),
            pltpu.VMEM((2 * HB, 1024), F32),
            pltpu.VMEM((16, 1024), F32),
            pltpu.VMEM((16, LANES), F32),
            pltpu.VMEM((4, 8, LANES), F32),
            pltpu.VMEM((GROUPS, LANES), F32),
            pltpu.VMEM((ROWS, GROUPS, LANES), F32),
            pltpu.VMEM((8, LANES), F32),
            pltpu.VMEM((ROWS, 8, LANES), F32),
            pltpu.VMEM((8, LANES), F32),
            pltpu.VMEM((PEERS, 8, LANES), F32),
            pltpu.SemaphoreType.DMA((MINE,)),
            pltpu.SemaphoreType.DMA((2,)),
            pltpu.SemaphoreType.DMA((2,)),
            pltpu.SemaphoreType.DMA((2,)),
            pltpu.SemaphoreType.DMA((2, MINE)),
            pltpu.SemaphoreType.DMA,
            pltpu.SemaphoreType.DMA,
            pltpu.SemaphoreType.DMA,
            pltpu.SemaphoreType.DMA,
            pltpu.SemaphoreType.DMA,
            pltpu.SemaphoreType.DMA,
        ],
        compiler_params=pltpu.CompilerParams(
            collective_id=0, has_side_effects=True, vmem_limit_bytes=60 * 2**20
        ),
        name="rotate",
    )(weights, left_bits, right_bits, groups, jnp.asarray(cosine_table()))
    return scaled, errors, scales, expert_error.reshape(1), total_error.reshape(())


def solution(mesh):
    placed = (P("expert", "row", None), P("expert", "row"), P("expert", None), P("expert", None))
    return jax.shard_map(
        body,
        mesh=mesh,
        in_specs=placed,
        out_specs=(
            P("expert", "row", None),
            P("expert", "row", None),
            P("expert", None),
            P("expert"),
            P(),
        ),
        check_vma=False,
    )
```

time: 256 us -> 107 us (0.42)
  waiting for transfers between devices: 98.9 us -> 0 us
  Pallas kernels: 0 us -> 96.5 us
  local copies, waits for them, and re-layouts: 63.1 us -> 5.89 us
  other arithmetic: 37 us -> 0 us
  starting transfers between devices: 26.7 us -> 0 us
  matrix products: 24.4 us -> 0 us
    all_to_all x5 -> x0, waiting for transfers between devices: 98.9 us -> none  [the longest x1 49.5 us: body(): lax.all_to_all(blocked, 'row', split_axis=3, concat_axis=1, tiled=True)]
    pallas_call x0 -> x1, Pallas kernels: none -> 96.5 us  [body(): pl.pallas_call(kernel, out_shape=(jax.ShapeDtypeStruct((1, MINE * HB, FF)...]
    convert_element_type x6 -> x0, local copies, waits for them, and re-layouts: 47.3 us -> none  [the longest x4 34.1 us: body(): rotated = lax.all_to_all(turned.astype(jnp.bfloat16), 'row', split_axis=1...]
    all_to_all x5 -> x0, starting transfers between devices: 26.7 us -> none  [the longest x3 15.7 us: from_everyone(): lax.all_to_all(jnp.broadcast_to(value[None], (peers, *value.shape)), axis...]
    dot_general x4 -> x0, matrix products: 24.4 us -> none  [the longest x1 9.8 us: row_transform(): jnp.einsum('eibf,bk->eikf', mixed_rows, row_hadamard, precision=lax.Preci...]
    reduce_sum x5 -> x0, other arithmetic: 22.7 us -> none  [the longest x1 19.5 us: coset_error(): parity = jnp.mod(jnp.sum(nearest, axis=-1), 2.0)]
    all_to_all x2 -> x0, local copies, waits for them, and re-layouts: 10.8 us -> none  [body(): lax.all_to_all(blocked, 'row', split_axis=3, concat_axis=1, tiled=True)]
    convert_element_type x3 -> x0, other arithmetic: 7.33 us -> none  [the longest x1 5.92 us: body(): scaled = values.astype(jnp.bfloat16)]
  transfers between devices with their start and end apart: 5 -> 0, of which waited for: 4 -> 0; matrix products, arithmetic and copies ran while one was open for 16% -> 0% of each run, Pallas kernels for 0% -> 0%
where the time goes in v1:
time: 107 us
  Pallas kernels  96.5 us (90%)
  local copies, waits for them, and re-layouts  5.89 us (6%)
  between operations  4.18 us (4%)
    pallas_call x1, Pallas kernels, body(): pl.pallas_call(kernel, out_shape=(jax.ShapeDtypeStruct((1, MINE * HB, FF)...  96.5 us
    unnamed x7, local copies, waits for them, and re-layouts  5.89 us

profile of v1, /device:TPU:0, one launch (start us, length us, event | category | flops | bytes accessed | tf_op | source)
XLA Modules:
  0.0 106.6 jit_solution(1890978503665556826)
XLA Ops:
  0.6 96.5 %rotate.1 = (bf16[1,896,2048]{2,1,0:T(8,128)(2,1)}, f32[1,896,256]{2,1,0:T(8,128)}, f32[1,16]{1,0:T(1,128)}, f32[1,1]{1,0:T(1,128)}, f32[1,1]{1,0:T(1,128)}) custom-call(bf16[1,896,2048]{2,1,0:T(8,128)(2,1)} %w_ref.1, s32[1,896]{1,0:T(1,128)} %lb_ref.1, s32[1,2048]{1,0:T(1,128)} %rb_ref.1, s32[1,2048]{1,0:T(1,128)} %g_ref.1, ...), custom_call_target="tpu_custom_call" | custom-call | tf_op jit(solution)/shard_map/rotate/pallas_call | solution.py:334
  97.2 0.0 copy-start
  97.2 0.0 copy-start.1
  97.2 4.5 %copy.15 = bf16[1,896,2048]{2,1,0:T(8,128)(2,1)} copy(bf16[1,896,2048]{2,1,0:T(8,128)(2,1)} %get-tuple-element.20) | data formatting | bytes 7340032
  101.6 0.0 copy-done
  101.7 0.9 copy.16
  102.6 0.0 copy-done.1
  102.6 0.5 copy.17
Async XLA Ops:
  97.2 4.5 %copy-start = (f32[1,896,256]{2,1,0:T(8,128)S(1)}, f32[1,896,256]{2,1,0:T(8,128)}, u32[]{:S(2)}) copy-start(f32[1,896,256]{2,1,0:T(8,128)} %get-tuple-element.21) | copy-start | bytes 2752516
  97.2 5.4 %copy-start.1 = (f32[1,16]{1,0:T(1,128)S(1)}, f32[1,16]{1,0:T(1,128)}, u32[]{:S(2)}) copy-start(f32[1,16]{1,0:T(1,128)} %get-tuple-element.22) | copy-start | bytes 196

commit v2 on v1

v2 whole, which is shorter than its diff:
```python
import math

import jax
import jax.numpy as jnp
import ml_dtypes
import numpy as np
from jax import lax
from jax.experimental import pallas as pl
from jax.experimental.pallas import tpu as pltpu
from jax.sharding import PartitionSpec as P

D = 7168
FF = 2048
HB = 128
GROUPS = 16
BLOCKS = 56
ROWS = 8
PEERS = 16
MINE = BLOCKS // ROWS
LANES = 128
MESH = pl.DeviceIdType.MESH
TOTAL_ORDER = (8, 1, 2, 4)
FIRST = 2
MIDDLE = 4
VMEM_LIMIT = 56 * 2**20
F32 = jnp.float32
BF16 = jnp.bfloat16


def cosine_table():
    first = np.arange(BLOCKS, dtype=np.float64)[:, None]
    second = np.arange(BLOCKS, dtype=np.float64)[None, :]
    table = math.sqrt(2.0 / BLOCKS) * np.cos(math.pi * (2.0 * second + 1.0) * first / (2.0 * BLOCKS))
    table[0] *= math.sqrt(0.5)
    padded = np.zeros((64, LANES), np.float32)
    padded[:BLOCKS, :BLOCKS] = table
    return padded.astype(ml_dtypes.bfloat16)


def iota(shape, dim):
    return lax.broadcasted_iota(jnp.int32, shape, dim)


def sign_of(common, bits):
    parity = common
    shift = bits // 2
    while shift:
        parity = jnp.bitwise_xor(parity, jnp.right_shift(parity, shift))
        shift //= 2
    return (1 - 2 * jnp.bitwise_and(parity, 1)).astype(F32)


def butterfly(parts):
    parts = list(parts)
    step = 1
    while step < len(parts):
        for low in range(len(parts)):
            if not low & step:
                a, b = parts[low], parts[low + step]
                parts[low], parts[low + step] = a + b, a - b
        step *= 2
    return parts


def odd(count):
    return count - 2.0 * jnp.floor(count * 0.5) > 0.5


def lattice(values):
    first = None
    for value in values:
        whole = jnp.floor(value)
        g = jnp.abs((value - whole) - 0.5)
        near = jnp.floor(value + 0.5)
        now = (g, g * g, g, g, whole, near)
        if first is None:
            first = now
        else:
            first = (
                first[0] + now[0],
                first[1] + now[1],
                jnp.maximum(first[2], g),
                jnp.minimum(first[3], g),
                first[4] + whole,
                first[5] + near,
            )
    total, squares, most, least, halves, wholes = first
    shifted = jnp.where(odd(halves), squares + 1.0 - 2.0 * most, squares)
    plain = 2.0 - total + squares
    plain = jnp.where(odd(wholes), plain + 2.0 * least, plain)
    return jnp.minimum(plain, shifted)


def push(src, dst, send, recv, device):
    pltpu.make_async_remote_copy(src, dst, send, recv, device_id=device, device_id_type=MESH).start()


def arrived(ref, sem):
    pltpu.make_async_copy(ref, ref, sem).wait()


def finish_block(blocks, perm, ybuf, natural, permuted, put_scaled, put_errors):
    ybuf[:HB, :] = jnp.dot(jnp.concatenate(blocks, axis=1), perm[...], preferred_element_type=F32)
    for k in range(ROWS):
        put_scaled(k, (blocks[k].astype(F32) * natural[k]).astype(BF16))

    def rows(r, carry):
        at = pl.ds(pl.multiple_of(r * 8, 8), 8)
        put_errors(r, lattice([ybuf[at, s * LANES:(s + 1) * LANES] * permuted[s] for s in range(8)]))
        return carry

    lax.fori_loop(0, HB // 8, rows, 0, unroll=4)


def rotate_kernel(
    w_ref, lb_ref, rb_ref, g_ref, cos_ref,
    scaled_ref, err_ref, small_ref, last_ref, perm, cs_nat, cs_perm,
    wv, lb, rb, gv, cosv, had, mix, right, left, signed, inner, sb1, rb1, mid, rot, rb2, ybuf,
    gperm, pk_s, pk_r, e_s, e_r, t_s, t_r,
    w_sem, in_sem, s1_send, s1_recv, s2_send, s2_recv, pk_send, pk_recv, e_send, e_recv, t_send, t_recv,
):
    me = lax.axis_index("row")
    ex = lax.axis_index("expert")
    row_peer = [lax.rem(me + k, ROWS) for k in range(1, ROWS)]
    ex_peer = [jnp.bitwise_xor(ex, bit) for bit in TOTAL_ORDER]

    small_loads = [
        pltpu.make_async_copy(src, dst, in_sem.at[n])
        for n, (src, dst) in enumerate(((lb_ref, lb), (rb_ref, rb), (g_ref, gv), (cos_ref, cosv)))
    ]
    loads = [
        pltpu.make_async_copy(w_ref.at[0, pl.ds(i * HB, HB)], wv.at[pl.ds(i * HB, HB)], w_sem.at[i])
        for i in range(MINE)
    ]
    for load in small_loads[:2] + loads[:1]:
        load.start()
    barrier = pltpu.get_barrier_semaphore()
    for p in row_peer:
        pl.semaphore_signal(barrier, inc=1, device_id={"row": p}, device_id_type=MESH)
    for p in ex_peer:
        pl.semaphore_signal(barrier, inc=1, device_id={"expert": p}, device_id_type=MESH)
    for load in loads[1:] + small_loads[2:]:
        load.start()

    had[...] = sign_of(jnp.bitwise_and(iota((256, 256), 0), iota((256, 256), 1)), 8).astype(BF16)
    small_loads[0].wait()
    small_loads[1].wait()
    right[...] = jnp.broadcast_to((2 * rb[...] - 1).astype(F32), (16, FF)).astype(BF16)

    def left_signs(i, carry):
        signs = (2 * lb[:, pl.ds(pl.multiple_of(i * HB, HB), HB)] - 1).astype(F32)
        left[i] = jnp.broadcast_to(signs, (HB, LANES)).T.astype(BF16)
        return carry

    left_signs(0, 0)

    def column_block(i):
        first = pl.multiple_of(i * HB, HB)
        lefts = jnp.concatenate([left[i], left[i]], axis=1)
        for p in range(8):
            x = wv[pl.ds(first, HB), p * 256:(p + 1) * 256]
            signed[p * HB:(p + 1) * HB, :] = x * lefts * right[0:1, p * 256:(p + 1) * 256]
        inner[...] = jnp.dot(signed[...], had[...], preferred_element_type=F32)
        for u in range(2):
            for r in range(HB // 16):
                parts = [inner[p * HB + r * 16:p * HB + (r + 1) * 16, u * LANES:(u + 1) * LANES] for p in range(8)]
                for t, part in enumerate(butterfly(parts)):
                    sb1[t // 4, (t % 4) * 2 + u, i, r * 16:(r + 1) * 16, :] = (part * (1.0 / math.sqrt(FF))).astype(BF16)

    def send_columns(i):
        for p in row_peer:
            push(sb1.at[0, p, i], rb1.at[0, me, i], s1_send.at[0], s1_recv.at[0], {"row": p})

    loads[0].wait()
    column_block(0)
    pl.semaphore_wait(barrier, ROWS - 1 + len(TOTAL_ORDER))
    send_columns(0)
    lax.fori_loop(1, MINE, left_signs, 0)

    def column_step(i, carry):
        pltpu.make_async_copy(w_ref.at[0, pl.ds(0, HB)], wv.at[pl.ds(0, HB)], w_sem.at[i]).wait()
        column_block(i)
        send_columns(i)
        return carry

    lax.fori_loop(1, MINE, column_step, 0)
    for p in row_peer:
        push(sb1.at[1, p], rb1.at[1, me], s1_send.at[1], s1_recv.at[1], {"row": p})
    for h in range(2):
        rb1[h, me] = sb1[h, me]

    small_loads[2].wait()
    small_loads[3].wait()
    pick_a = (jnp.right_shift(iota((896, 64), 0), 4) == iota((896, 64), 1)).astype(F32).astype(BF16)
    spread = jnp.dot(pick_a, cosv[...], preferred_element_type=F32).astype(BF16)
    pick_j = (jnp.right_shift(iota((LANES, 896), 1), 4) == iota((LANES, 896), 0)).astype(F32).astype(BF16)
    mix[...] = jnp.dot(spread, pick_j, preferred_element_type=F32).astype(BF16)
    small = sign_of(
        jnp.bitwise_and(jnp.bitwise_and(iota((16, 896), 0), iota((16, 896), 1)), 15), 4
    ).astype(BF16)

    def sign_mix(a, carry):
        at = pl.ds(pl.multiple_of(a * 16, 16), 16)
        mix[at, :] = mix[at, :] * small
        return carry

    lax.fori_loop(0, BLOCKS, sign_mix, 0)
    for s in range(8):
        perm[:, s * LANES:(s + 1) * LANES] = (
            iota((1024, LANES), 0) == 8 * iota((1024, LANES), 1) + s
        ).astype(F32).astype(BF16)
    which = iota((16, 1024), 0)
    ids = jnp.zeros((16, 1024), F32)
    for h in range(2):
        ids = jnp.where(which == h, gv[:, h * 1024:(h + 1) * 1024].astype(F32), ids)
        own = gv[:, pl.ds(pl.multiple_of(h * 1024 + me * LANES, LANES), LANES)].astype(F32)
        ids = jnp.where(which == 2 + h, jnp.concatenate([own] * 8, axis=1), ids)
    gperm[...] = jnp.dot(ids.astype(BF16), perm[...], preferred_element_type=F32)

    def rotate_rows(h):
        arrived(rb1.at[h, pl.ds(0, ROWS - 1)], s1_recv.at[h])

        def mix_blocks(q, carry):
            parts = []
            for half in range(2):
                at = pl.ds(pl.multiple_of(q * 32 + half * 16, 16), 16)
                parts.append(rb1[h, :, :, at, :].reshape(896, LANES))
            out = jnp.dot(mix[...], jnp.concatenate(parts, axis=1), preferred_element_type=F32)
            mid[2 * q] = out[:, :LANES]
            mid[2 * q + 1] = out[:, LANES:]
            return carry

        lax.fori_loop(0, 4, mix_blocks, 0)

        def turn(a, peak):
            at = pl.ds(pl.multiple_of(a * 16, 16), 16)
            parts = butterfly([mid[q, at, :] for q in range(8)])
            for q, part in enumerate(parts):
                part = part * (1.0 / math.sqrt(HB))
                peak = jnp.maximum(peak, jnp.abs(part))
                rot[h, a // MINE, lax.rem(a, MINE), q * 16:(q + 1) * 16, :] = part.astype(BF16)
            return peak

        peak = lax.fori_loop(0, BLOCKS, turn, jnp.zeros((16, LANES), F32))
        rb2[h, me] = rot[h, me]
        return jnp.max(peak, axis=0, keepdims=True)

    def send_rows(h, blocks):
        for i in blocks:
            for p in row_peer:
                push(rot.at[h, p, i], rb2.at[h, me, i], s2_send.at[h], s2_recv.at[h, i], {"row": p})

    def to_row(slots, own, source, send, recv):
        slots[me] = own
        source[...] = own
        for p in row_peer:
            push(source, slots.at[me], send, recv, {"row": p})

    col_peak = [rotate_rows(0)]
    send_rows(0, range(0, FIRST))
    col_peak.append(rotate_rows(1))

    group_id = iota((GROUPS, LANES), 0)
    most = jnp.zeros((GROUPS, LANES), F32)
    for h in range(2):
        own = gv[:, pl.ds(pl.multiple_of(h * 1024 + me * LANES, LANES), LANES)]
        most = jnp.maximum(most, jnp.where(group_id == own, col_peak[h], 0.0))
    most = jnp.broadcast_to(jnp.max(most, axis=1, keepdims=True), (GROUPS, LANES))
    to_row(pk_r, most, pk_s, pk_send, pk_recv)
    send_rows(0, range(FIRST, MINE))

    arrived(pk_r.at[pl.ds(0, ROWS - 1)], pk_recv)
    group_peak = jnp.ones((GROUPS, LANES), F32)
    for k in range(ROWS):
        group_peak = jnp.maximum(group_peak, pk_r[k])
    small_ref[0:1, :] = jnp.sum(
        jnp.where(group_id == iota((GROUPS, LANES), 1), group_peak * 0.5, 0.0), axis=0, keepdims=True
    )
    inverse = 2.0 / group_peak
    for m in range(16):
        ids = gv[:, m * LANES:(m + 1) * LANES]
        cs_nat[m:m + 1, :] = jnp.sum(jnp.where(group_id == ids, inverse, 0.0), axis=0, keepdims=True)
    for k in range(4):
        for s in range(8):
            ids = gperm[k:k + 1, s * LANES:(s + 1) * LANES]
            cs_perm[k, s:s + 1, :] = jnp.sum(
                jnp.where(group_id.astype(F32) == ids, inverse, 0.0), axis=0, keepdims=True
            )

    def own_errors(n, total):
        parts = []
        for h in range(2):
            blocks = []
            for k in range(8):
                a = n * 8 + k
                blocks.append(rot[h, a // MINE, lax.rem(a, MINE)])
            parts.append(jnp.concatenate(blocks, axis=1))
        ybuf[...] = jnp.dot(jnp.concatenate(parts, axis=0), perm[...], preferred_element_type=F32)
        block = n * 8 + jnp.right_shift(iota((8, LANES), 1), 4)
        for h in range(2):
            scales = [cs_perm[2 + h, s:s + 1, :] for s in range(8)]

            def rows(r, total):
                at = pl.ds(pl.multiple_of(h * HB + r * 8, 8), 8)
                errors = lattice([ybuf[at, s * LANES:(s + 1) * LANES] * scales[s] for s in range(8)])
                row = (block * HB + r * 8 + iota((8, LANES), 0)).astype(F32)
                return total + errors * ((1.0 + 4.0 * (row + 0.5) / D) / 3.0)

            total = lax.fori_loop(0, HB // 8, rows, total, unroll=4)
        return total

    error = lax.fori_loop(0, MIDDLE, own_errors, jnp.zeros((8, LANES), F32))
    send_rows(1, range(0, 1))
    error = lax.fori_loop(MIDDLE, MINE, own_errors, error)
    to_row(e_r, error, e_s, e_send, e_recv)
    send_rows(1, range(1, 2))

    def finish(h, start, stop):
        def step(i, carry):
            arrived(rb2.at[h, pl.ds(0, ROWS - 1), i], s2_recv.at[h, i])
            first = pl.multiple_of(i * HB, HB)

            def put_scaled(k, value):
                scaled_ref[0, pl.ds(first, HB), (h * 8 + k) * LANES:(h * 8 + k + 1) * LANES] = value

            def put_errors(r, value):
                err_ref[0, pl.ds(pl.multiple_of(first + r * 8, 8), 8), h * LANES:(h + 1) * LANES] = value

            finish_block(
                [rb2[h, k, i] for k in range(ROWS)], perm, ybuf,
                [cs_nat[h * 8 + k:h * 8 + k + 1, :] for k in range(ROWS)],
                [cs_perm[h, s:s + 1, :] for s in range(8)], put_scaled, put_errors,
            )
            return carry

        lax.fori_loop(start, stop, step, 0)

    finish(0, 0, 2)
    arrived(e_r.at[pl.ds(0, ROWS - 1)], e_recv)
    error = e_r[0]
    for k in range(1, ROWS):
        error = error + e_r[k]
    error = jnp.sum(jnp.sum(error, axis=1, keepdims=True), axis=0, keepdims=True) * (1.0 / (D * FF // 8))
    total = jnp.broadcast_to(error, (8, LANES))
    small_ref[1:2, :] = total[:1]
    done = 2
    for n, p in enumerate(ex_peer):
        t_s[n] = total
        push(t_s.at[n], t_r.at[n], t_send.at[n], t_recv.at[n], {"expert": p})
        send_rows(1, range(2 + n, 3 + n) if n < 3 else range(5, MINE))
        more = 2 if n == 0 else 1
        finish(0, done, done + more)
        done += more
        arrived(t_r.at[n], t_recv.at[n])
        total = total + t_r[n]
    small_ref[2:3, :] = total[:1] * (1.0 / PEERS)
    finish(1, 0, MINE - 1)
    arrived(rb2.at[1, pl.ds(0, ROWS - 1), MINE - 1], s2_recv.at[1, MINE - 1])
    for k in range(ROWS):
        last_ref[k] = rb2[1, k, MINE - 1]

    for h in range(2):
        arrived(sb1.at[h, pl.ds(0, ROWS - 1)], s1_send.at[h])
        arrived(rot.at[h, pl.ds(0, ROWS - 1)], s2_send.at[h])
    arrived(pk_r.at[pl.ds(0, ROWS - 1)], pk_send)
    arrived(e_r.at[pl.ds(0, ROWS - 1)], e_send)
    for n in range(len(TOTAL_ORDER)):
        arrived(t_s.at[n], t_send.at[n])


def finish_kernel(
    scaled, errors, small, last, perm, cs_nat, cs_perm,
    scaled_ref, err_ref, scale_ref, expert_ref, total_ref,
    ybuf, scaled_last, err_last, sems,
):
    edge = (MINE - 1) * HB
    half = FF // 2
    copies = [
        pltpu.make_async_copy(scaled.at[:, pl.ds(0, edge)], scaled_ref.at[:, pl.ds(0, edge)], sems.at[0]),
        pltpu.make_async_copy(
            scaled.at[:, pl.ds(edge, HB), pl.ds(0, half)], scaled_ref.at[:, pl.ds(edge, HB), pl.ds(0, half)], sems.at[1]
        ),
        pltpu.make_async_copy(errors.at[:, pl.ds(0, edge)], err_ref.at[:, pl.ds(0, edge)], sems.at[2]),
        pltpu.make_async_copy(
            errors.at[:, pl.ds(edge, HB), pl.ds(0, LANES)], err_ref.at[:, pl.ds(edge, HB), pl.ds(0, LANES)], sems.at[3]
        ),
    ]
    for copy in copies:
        copy.start()
    scale_ref[...] = small[0:1, :GROUPS]
    expert_ref[...] = small[1:2, :1]
    total_ref[...] = small[2:3, :1]

    def put_scaled(k, value):
        scaled_last[0, :, k * LANES:(k + 1) * LANES] = value

    def put_errors(r, value):
        err_last[0, pl.ds(pl.multiple_of(r * 8, 8), 8), :] = value

    finish_block(
        [last[k] for k in range(ROWS)], perm, ybuf,
        [cs_nat[8 + k:9 + k, :] for k in range(ROWS)],
        [cs_perm[1, s:s + 1, :] for s in range(8)], put_scaled, put_errors,
    )
    rest = [
        pltpu.make_async_copy(scaled_last, scaled_ref.at[:, pl.ds(edge, HB), pl.ds(half, half)], sems.at[4]),
        pltpu.make_async_copy(err_last, err_ref.at[:, pl.ds(edge, HB), pl.ds(LANES, LANES)], sems.at[5]),
    ]
    for copy in rest:
        copy.start()
    for copy in copies + rest:
        copy.wait()


def body(weights, left_bits, right_bits, groups):
    vmem = pl.BlockSpec(memory_space=pltpu.VMEM)
    hbm = pl.BlockSpec(memory_space=pltpu.HBM)
    rows = MINE * HB
    dma = pltpu.SemaphoreType.DMA
    arguments = [
        pltpu.with_memory_space_constraint(x, pltpu.HBM)
        for x in (weights, left_bits, right_bits, groups, jnp.asarray(cosine_table()))
    ]
    parts = pl.pallas_call(
        rotate_kernel,
        out_shape=(
            pltpu.VMEM((1, rows, FF), BF16),
            pltpu.VMEM((1, rows, FF // 8), F32),
            pltpu.VMEM((8, LANES), F32),
            pltpu.VMEM((ROWS, HB, LANES), BF16),
            pltpu.VMEM((1024, 1024), BF16),
            pltpu.VMEM((16, LANES), F32),
            pltpu.VMEM((4, 8, LANES), F32),
        ),
        in_specs=[hbm] * 5,
        out_specs=(vmem,) * 7,
        scratch_shapes=[
            pltpu.VMEM((rows, FF), BF16),
            pltpu.VMEM((1, rows), jnp.int32),
            pltpu.VMEM((1, FF), jnp.int32),
            pltpu.VMEM((1, FF), jnp.int32),
            pltpu.VMEM((64, LANES), BF16),
            pltpu.VMEM((256, 256), BF16),
            pltpu.VMEM((896, 896), BF16),
            pltpu.VMEM((16, FF), BF16),
            pltpu.VMEM((MINE, HB, LANES), BF16),
            pltpu.VMEM((8 * HB, 256), BF16),
            pltpu.VMEM((8 * HB, 256), F32),
            pltpu.VMEM((2, ROWS, MINE, HB, LANES), BF16),
            pltpu.VMEM((2, ROWS, MINE, HB, LANES), BF16),
            pltpu.VMEM((8, 896, LANES), F32),
            pltpu.VMEM((2, ROWS, MINE, HB, LANES), BF16),
            pltpu.VMEM((2, ROWS, MINE, HB, LANES), BF16),
            pltpu.VMEM((2 * HB, 1024), F32),
            pltpu.VMEM((16, 1024), F32),
            pltpu.VMEM((GROUPS, LANES), F32),
            pltpu.VMEM((ROWS, GROUPS, LANES), F32),
            pltpu.VMEM((8, LANES), F32),
            pltpu.VMEM((ROWS, 8, LANES), F32),
            pltpu.VMEM((len(TOTAL_ORDER), 8, LANES), F32),
            pltpu.VMEM((len(TOTAL_ORDER), 8, LANES), F32),
            dma((MINE,)),
            dma((4,)),
            dma((2,)),
            dma((2,)),
            dma((2,)),
            dma((2, MINE)),
            dma,
            dma,
            dma,
            dma,
            dma((len(TOTAL_ORDER),)),
            dma((len(TOTAL_ORDER),)),
        ],
        compiler_params=pltpu.CompilerParams(
            collective_id=0, has_side_effects=True, vmem_limit_bytes=VMEM_LIMIT
        ),
        name="rotate",
    )(*arguments)
    scaled, errors, scales, expert_error, total_error = pl.pallas_call(
        finish_kernel,
        out_shape=(
            jax.ShapeDtypeStruct((1, rows, FF), BF16),
            jax.ShapeDtypeStruct((1, rows, FF // 8), F32),
            jax.ShapeDtypeStruct((1, GROUPS), F32),
            jax.ShapeDtypeStruct((1, 1), F32),
            jax.ShapeDtypeStruct((1, 1), F32),
        ),
        in_specs=[vmem] * 7,
        out_specs=(hbm, hbm, vmem, vmem, vmem),
        scratch_shapes=[
            pltpu.VMEM((HB, 1024), F32),
            pltpu.VMEM((1, HB, FF // 2), BF16),
            pltpu.VMEM((1, HB, LANES), F32),
            dma((6,)),
        ],
        compiler_params=pltpu.CompilerParams(vmem_limit_bytes=8 * 2**20),
        name="finish",
    )(*parts)
    return scaled, errors, scales, expert_error.reshape(1), total_error.reshape(())


def solution(mesh):
    placed = (P("expert", "row", None), P("expert", "row"), P("expert", None), P("expert", None))
    return jax.shard_map(
        body,
        mesh=mesh,
        in_specs=placed,
        out_specs=(
            P("expert", "row", None),
            P("expert", "row", None),
            P("expert", None),
            P("expert"),
            P(),
        ),
        check_vma=False,
    )
```

time: 107 us -> 95.9 us (0.90)
  local copies, waits for them, and re-layouts: 5.89 us -> 0 us
  between operations: 4.18 us -> 0.64 us
  Pallas kernels: 96.5 us -> 95 us
    unnamed x7 -> x0, local copies, waits for them, and re-layouts: 5.89 us -> none
    pallas_call x1 -> x2, Pallas kernels: 96.5 us -> 95 us  [the longest x1 92.3 us: body(): pl.pallas_call(rotate_kernel, out_shape=(pltpu.VMEM((1, rows, FF), BF16),...]
where the time goes in v2:
time: 95.9 us; the launch traced here: 95.7 us
  Pallas kernels  95 us (99%)
    pallas_call x1, Pallas kernels, body(): pl.pallas_call(rotate_kernel, out_shape=(pltpu.VMEM((1, rows, FF), BF16),...  92.3 us
    pallas_call x1, Pallas kernels, body(): pl.pallas_call(finish_kernel, out_shape=(jax.ShapeDtypeStruct((1, rows, F...  2.78 us

profile of v2, /device:TPU:0, one launch (start us, length us, event | category | flops | bytes accessed | tf_op | source)
XLA Modules:
  0.0 95.7 jit_solution(5975414987473593848)
XLA Ops:
  0.6 92.3 %rotate.1 = (bf16[1,896,2048]{2,1,0:T(8,128)(2,1)S(1)}, f32[1,896,256]{2,1,0:T(8,128)S(1)}, f32[8,128]{1,0:T(8,128)S(1)}, bf16[8,128,128]{2,1,0:T(8,128)(2,1)S(1...) custom-call(bf16[1,896,2048]{2,1,0:T(8,128)(2,1)} %w_ref.1, s32[1,896]{1,0:T(1,128)} %lb_ref.1, ...), custom_call_target="tpu_custom_call" | custom-call | tf_op jit(solution)/shard_map/rotate/pallas_call | solution.py:424
  92.9 2.8 %finish.1 = (bf16[1,896,2048]{2,1,0:T(8,128)(2,1)}, f32[1,896,256]{2,1,0:T(8,128)}, f32[1,16]{1,0:T(1,128)}, f32[1,1]{1,0:T(1,128)}, f32[1,1]{1,0:T(1,128)}) custom-call(bf16[1,896,2048]{2,1,0:T(8,128)(2,1)S(1)} %get-tuple-element.17.scaled, f32[1,896,256]{2,1,0:T(8,128)S(1)} %get-tuple-element.18.errors, f32[8,128]{1,0:T(8,128)S(1)} %get-tuple-element.19.small, ...), custom_call_target="tpu_custom_call" | custom-call | tf_op jit(solution)/shard_map/finish/pallas_call | solution.py:480

commit v3 on v2

--- a/solution.py
+++ b/solution.py
@@ -19,8 +19,8 @@
 MINE = BLOCKS // ROWS
 LANES = 128
 MESH = pl.DeviceIdType.MESH
-TOTAL_ORDER = (8, 1, 2, 4)
-FIRST = 2
+TOTAL_ORDER = ((8, 1), (1, 0), (2, 0), (4, 0))
+FIRST = 3
 MIDDLE = 4
 VMEM_LIMIT = 56 * 2**20
 F32 = jnp.float32
@@ -122,7 +122,9 @@
     me = lax.axis_index("row")
     ex = lax.axis_index("expert")
     row_peer = [lax.rem(me + k, ROWS) for k in range(1, ROWS)]
-    ex_peer = [jnp.bitwise_xor(ex, bit) for bit in TOTAL_ORDER]
+    ex_peer = [
+        {"expert": jnp.bitwise_xor(ex, ex_bit), "row": jnp.bitwise_xor(me, row_bit)} for ex_bit, row_bit in TOTAL_ORDER
+    ]
 
     small_loads = [
         pltpu.make_async_copy(src, dst, in_sem.at[n])
@@ -138,7 +140,7 @@
     for p in row_peer:
         pl.semaphore_signal(barrier, inc=1, device_id={"row": p}, device_id_type=MESH)
     for p in ex_peer:
-        pl.semaphore_signal(barrier, inc=1, device_id={"expert": p}, device_id_type=MESH)
+        pl.semaphore_signal(barrier, inc=1, device_id=p, device_id_type=MESH)
     for load in loads[1:] + small_loads[2:]:
         load.start()
 
@@ -310,10 +312,9 @@
         return total
 
     error = lax.fori_loop(0, MIDDLE, own_errors, jnp.zeros((8, LANES), F32))
-    send_rows(1, range(0, 1))
     error = lax.fori_loop(MIDDLE, MINE, own_errors, error)
     to_row(e_r, error, e_s, e_send, e_recv)
-    send_rows(1, range(1, 2))
+    send_rows(1, range(0, MINE))
 
     def finish(h, start, stop):
         def step(i, carry):
@@ -346,8 +347,7 @@
     done = 2
     for n, p in enumerate(ex_peer):
         t_s[n] = total
-        push(t_s.at[n], t_r.at[n], t_send.at[n], t_recv.at[n], {"expert": p})
-        send_rows(1, range(2 + n, 3 + n) if n < 3 else range(5, MINE))
+        push(t_s.at[n], t_r.at[n], t_send.at[n], t_recv.at[n], p)
         more = 2 if n == 0 else 1
         finish(0, done, done + more)
         done += more

time: 95.9 us -> 93 us (0.970)
  Pallas kernels: 95 us -> 92.2 us
    pallas_call x1, Pallas kernels: 92.3 us -> 89.4 us  [body(): pl.pallas_call(rotate_kernel, out_shape=(pltpu.VMEM((1, rows, FF), BF16),...]
where the time goes in v3:
time: 93 us; the launch traced here: 92.9 us
  Pallas kernels  92.2 us (99%)
    pallas_call x1, Pallas kernels, body(): pl.pallas_call(rotate_kernel, out_shape=(pltpu.VMEM((1, rows, FF), BF16),...  89.4 us
    pallas_call x1, Pallas kernels, body(): pl.pallas_call(finish_kernel, out_shape=(jax.ShapeDtypeStruct((1, rows, F...  2.78 us

profile of v3, /device:TPU:0, one launch (start us, length us, event | category | flops | bytes accessed | tf_op | source)
XLA Modules:
  0.0 92.9 jit_solution(13248137103546481805)
XLA Ops:
  0.6 89.4 %rotate.1 = (bf16[1,896,2048]{2,1,0:T(8,128)(2,1)S(1)}, f32[1,896,256]{2,1,0:T(8,128)S(1)}, f32[8,128]{1,0:T(8,128)S(1)}, bf16[8,128,128]{2,1,0:T(8,128)(2,1)S(1...) custom-call(bf16[1,896,2048]{2,1,0:T(8,128)(2,1)} %w_ref.1, s32[1,896]{1,0:T(1,128)} %lb_ref.1, ...), custom_call_target="tpu_custom_call" | custom-call | tf_op jit(solution)/shard_map/rotate/pallas_call | solution.py:424
  90.1 2.8 %finish.1 = (bf16[1,896,2048]{2,1,0:T(8,128)(2,1)}, f32[1,896,256]{2,1,0:T(8,128)}, f32[1,16]{1,0:T(1,128)}, f32[1,1]{1,0:T(1,128)}, f32[1,1]{1,0:T(1,128)}) custom-call(bf16[1,896,2048]{2,1,0:T(8,128)(2,1)S(1)} %get-tuple-element.17.scaled, f32[1,896,256]{2,1,0:T(8,128)S(1)} %get-tuple-element.18.errors, f32[8,128]{1,0:T(8,128)S(1)} %get-tuple-element.19.small, ...), custom_call_target="tpu_custom_call" | custom-call | tf_op jit(solution)/shard_map/finish/pallas_call | solution.py:480

commit v4 on v3

--- a/solution.py
+++ b/solution.py
@@ -109,7 +109,7 @@
         put_errors(r, lattice([ybuf[at, s * LANES:(s + 1) * LANES] * permuted[s] for s in range(8)]))
         return carry
 
-    lax.fori_loop(0, HB // 8, rows, 0, unroll=4)
+    lax.fori_loop(0, HB // 8, rows, 0, unroll=8)
 
 
 def rotate_kernel(
@@ -117,11 +117,14 @@
     scaled_ref, err_ref, small_ref, last_ref, perm, cs_nat, cs_perm,
     wv, lb, rb, gv, cosv, had, mix, right, left, signed, inner, sb1, rb1, mid, rot, rb2, ybuf,
     gperm, pk_s, pk_r, e_s, e_r, t_s, t_r,
-    w_sem, in_sem, s1_send, s1_recv, s2_send, s2_recv, pk_send, pk_recv, e_send, e_recv, t_send, t_recv,
+    here, w_sem, in_sem, s1_send, s1_recv, s2_send, s2_recv, pk_send, pk_recv, e_send, e_recv, t_send, t_recv,
 ):
     me = lax.axis_index("row")
     ex = lax.axis_index("expert")
-    row_peer = [lax.rem(me + k, ROWS) for k in range(1, ROWS)]
+    row_peer = [
+        lax.rem(jnp.right_shift(me, 1) + dz, 4) * 2 + jnp.bitwise_xor(jnp.bitwise_and(me, 1), dx)
+        for dz, dx in ((2, 1), (2, 0), (1, 1), (3, 1), (1, 0), (3, 0), (0, 1))
+    ]
     ex_peer = [
         {"expert": jnp.bitwise_xor(ex, ex_bit), "row": jnp.bitwise_xor(me, row_bit)} for ex_bit, row_bit in TOTAL_ORDER
     ]
@@ -139,8 +142,13 @@
     barrier = pltpu.get_barrier_semaphore()
     for p in row_peer:
         pl.semaphore_signal(barrier, inc=1, device_id={"row": p}, device_id_type=MESH)
-    for p in ex_peer:
-        pl.semaphore_signal(barrier, inc=1, device_id=p, device_id_type=MESH)
+    higher = [jnp.bitwise_and(ex, ex_bit) != 0 for ex_bit, _ in TOTAL_ORDER]
+    for p, high in zip(ex_peer, higher):
+
+        @pl.when(jnp.logical_not(high))
+        def _():
+            pl.semaphore_signal(barrier, inc=1, device_id=p, device_id_type=MESH)
+
     for load in loads[1:] + small_loads[2:]:
         load.start()
 
@@ -175,7 +183,7 @@
 
     loads[0].wait()
     column_block(0)
-    pl.semaphore_wait(barrier, ROWS - 1 + len(TOTAL_ORDER))
+    pl.semaphore_wait(barrier, ROWS - 1 + sum(high.astype(jnp.int32) for high in higher))
     send_columns(0)
     lax.fori_loop(1, MINE, left_signs, 0)
 
@@ -188,6 +196,12 @@
     lax.fori_loop(1, MINE, column_step, 0)
     for p in row_peer:
         push(sb1.at[1, p], rb1.at[1, me], s1_send.at[1], s1_recv.at[1], {"row": p})
+    for n, (p, high) in enumerate(zip(ex_peer, higher)):
+
+        @pl.when(high)
+        def _():
+            pl.semaphore_signal(here.at[n], inc=1, device_id=p, device_id_type=MESH)
+
     for h in range(2):
         rb1[h, me] = sb1[h, me]
 
@@ -243,7 +257,7 @@
                 rot[h, a // MINE, lax.rem(a, MINE), q * 16:(q + 1) * 16, :] = part.astype(BF16)
             return peak
 
-        peak = lax.fori_loop(0, BLOCKS, turn, jnp.zeros((16, LANES), F32))
+        peak = lax.fori_loop(0, BLOCKS, turn, jnp.zeros((16, LANES), F32), unroll=4)
         rb2[h, me] = rot[h, me]
         return jnp.max(peak, axis=0, keepdims=True)
 
@@ -289,30 +303,30 @@
                 jnp.where(group_id.astype(F32) == ids, inverse, 0.0), axis=0, keepdims=True
             )
 
-    def own_errors(n, total):
+    def reorder(n):
         parts = []
         for h in range(2):
-            blocks = []
-            for k in range(8):
-                a = n * 8 + k
-                blocks.append(rot[h, a // MINE, lax.rem(a, MINE)])
+            blocks = [rot[h, (n * 8 + k) // MINE, (n * 8 + k) % MINE] for k in range(8)]
             parts.append(jnp.concatenate(blocks, axis=1))
-        ybuf[...] = jnp.dot(jnp.concatenate(parts, axis=0), perm[...], preferred_element_type=F32)
+        return jnp.dot(jnp.concatenate(parts, axis=0), perm[...], preferred_element_type=F32)
+
+    def own_errors(n, total):
         block = n * 8 + jnp.right_shift(iota((8, LANES), 1), 4)
         for h in range(2):
             scales = [cs_perm[2 + h, s:s + 1, :] for s in range(8)]
-
-            def rows(r, total):
-                at = pl.ds(pl.multiple_of(h * HB + r * 8, 8), 8)
-                errors = lattice([ybuf[at, s * LANES:(s + 1) * LANES] * scales[s] for s in range(8)])
+            for r in range(HB // 8):
+                at = slice(h * HB + r * 8, h * HB + r * 8 + 8)
+                errors = lattice([ybuf[n % 2, at, s * LANES:(s + 1) * LANES] * scales[s] for s in range(8)])
                 row = (block * HB + r * 8 + iota((8, LANES), 0)).astype(F32)
-                return total + errors * ((1.0 + 4.0 * (row + 0.5) / D) / 3.0)
-
-            total = lax.fori_loop(0, HB // 8, rows, total, unroll=4)
+                total = total + errors * ((1.0 + 4.0 * (row + 0.5) / D) / 3.0)
         return total
 
-    error = lax.fori_loop(0, MIDDLE, own_errors, jnp.zeros((8, LANES), F32))
-    error = lax.fori_loop(MIDDLE, MINE, own_errors, error)
+    error = jnp.zeros((8, LANES), F32)
+    ybuf[0] = reorder(0)
+    for n in range(MINE):
+        if n + 1 < MINE:
+            ybuf[(n + 1) % 2] = reorder(n + 1)
+        error = own_errors(n, error)
     to_row(e_r, error, e_s, e_send, e_recv)
     send_rows(1, range(0, MINE))
 
@@ -328,7 +342,7 @@
                 err_ref[0, pl.ds(pl.multiple_of(first + r * 8, 8), 8), h * LANES:(h + 1) * LANES] = value
 
             finish_block(
-                [rb2[h, k, i] for k in range(ROWS)], perm, ybuf,
+                [rb2[h, k, i] for k in range(ROWS)], perm, ybuf.at[0],
                 [cs_nat[h * 8 + k:h * 8 + k + 1, :] for k in range(ROWS)],
                 [cs_perm[h, s:s + 1, :] for s in range(8)], put_scaled, put_errors,
             )
@@ -336,7 +350,7 @@
 
         lax.fori_loop(start, stop, step, 0)
 
-    finish(0, 0, 2)
+    finish(0, 0, 4)
     arrived(e_r.at[pl.ds(0, ROWS - 1)], e_recv)
     error = e_r[0]
     for k in range(1, ROWS):
@@ -344,17 +358,19 @@
     error = jnp.sum(jnp.sum(error, axis=1, keepdims=True), axis=0, keepdims=True) * (1.0 / (D * FF // 8))
     total = jnp.broadcast_to(error, (8, LANES))
     small_ref[1:2, :] = total[:1]
-    done = 2
+    meanwhile = ((0, 4, MINE), (1, 0, 1), (1, 1, 2), (1, 2, MINE - 1))
     for n, p in enumerate(ex_peer):
         t_s[n] = total
+
+        @pl.when(jnp.logical_not(higher[n]))
+        def _():
+            pl.semaphore_wait(here.at[n], 1)
+
         push(t_s.at[n], t_r.at[n], t_send.at[n], t_recv.at[n], p)
-        more = 2 if n == 0 else 1
-        finish(0, done, done + more)
-        done += more
+        finish(*meanwhile[n])
         arrived(t_r.at[n], t_recv.at[n])
         total = total + t_r[n]
     small_ref[2:3, :] = total[:1] * (1.0 / PEERS)
-    finish(1, 0, MINE - 1)
     arrived(rb2.at[1, pl.ds(0, ROWS - 1), MINE - 1], s2_recv.at[1, MINE - 1])
     for k in range(ROWS):
         last_ref[k] = rb2[1, k, MINE - 1]
@@ -371,7 +387,7 @@
 def finish_kernel(
     scaled, errors, small, last, perm, cs_nat, cs_perm,
     scaled_ref, err_ref, scale_ref, expert_ref, total_ref,
-    ybuf, scaled_last, err_last, sems,
+    ybuf, scaled_last, err_last, scale_v, expert_v, total_v, sems,
 ):
     edge = (MINE - 1) * HB
     half = FF // 2
@@ -387,9 +403,12 @@
     ]
     for copy in copies:
         copy.start()
-    scale_ref[...] = small[0:1, :GROUPS]
-    expert_ref[...] = small[1:2, :1]
-    total_ref[...] = small[2:3, :1]
+    scale_v[...] = small[0:1, :GROUPS]
+    expert_v[...] = small[1:2, :1]
+    total_v[...] = small[2:3, :1]
+    for n, (src, dst) in enumerate(((scale_v, scale_ref), (expert_v, expert_ref), (total_v, total_ref))):
+        copies.append(pltpu.make_async_copy(src, dst, sems.at[6 + n]))
+        copies[-1].start()
 
     def put_scaled(k, value):
         scaled_last[0, :, k * LANES:(k + 1) * LANES] = value
@@ -451,7 +470,7 @@
             pltpu.VMEM((8, 896, LANES), F32),
             pltpu.VMEM((2, ROWS, MINE, HB, LANES), BF16),
             pltpu.VMEM((2, ROWS, MINE, HB, LANES), BF16),
-            pltpu.VMEM((2 * HB, 1024), F32),
+            pltpu.VMEM((2, 2 * HB, 1024), F32),
             pltpu.VMEM((16, 1024), F32),
             pltpu.VMEM((GROUPS, LANES), F32),
             pltpu.VMEM((ROWS, GROUPS, LANES), F32),
@@ -459,6 +478,7 @@
             pltpu.VMEM((ROWS, 8, LANES), F32),
             pltpu.VMEM((len(TOTAL_ORDER), 8, LANES), F32),
             pltpu.VMEM((len(TOTAL_ORDER), 8, LANES), F32),
+            pltpu.SemaphoreType.REGULAR((len(TOTAL_ORDER),)),
             dma((MINE,)),
             dma((4,)),
             dma((2,)),
@@ -487,12 +507,15 @@
             jax.ShapeDtypeStruct((1, 1), F32),
         ),
         in_specs=[vmem] * 7,
-        out_specs=(hbm, hbm, vmem, vmem, vmem),
+        out_specs=(hbm,) * 5,
         scratch_shapes=[
             pltpu.VMEM((HB, 1024), F32),
             pltpu.VMEM((1, HB, FF // 2), BF16),
             pltpu.VMEM((1, HB, LANES), F32),
-            dma((6,)),
+            pltpu.VMEM((1, GROUPS), F32),
+            pltpu.VMEM((1, 1), F32),
+            pltpu.VMEM((1, 1), F32),
+            dma((9,)),
         ],
         compiler_params=pltpu.CompilerParams(vmem_limit_bytes=8 * 2**20),
         name="finish",

time: 93 us -> 89.8 us (0.966)
  Pallas kernels: 92.2 us -> 89.1 us
    pallas_call x1, Pallas kernels: 89.4 us -> 86.9 us  [body(): pl.pallas_call(rotate_kernel, out_shape=(pltpu.VMEM((1, rows, FF), BF16),...]
where the time goes in v4:
time: 89.8 us; the launch traced here: 89.7 us
  Pallas kernels  89.1 us (99%)
    pallas_call x1, Pallas kernels, body(): pl.pallas_call(rotate_kernel, out_shape=(pltpu.VMEM((1, rows, FF), BF16),...  86.9 us
    pallas_call x1, Pallas kernels, body(): pl.pallas_call(finish_kernel, out_shape=(jax.ShapeDtypeStruct((1, rows, F...  2.2 us

profile of v4, /device:TPU:0, one launch (start us, length us, event | category | flops | bytes accessed | tf_op | source)
XLA Modules:
  0.0 89.7 jit_solution(5150183874106424878)
XLA Ops:
  0.6 86.9 %rotate.1 = (bf16[1,896,2048]{2,1,0:T(8,128)(2,1)S(1)}, f32[1,896,256]{2,1,0:T(8,128)S(1)}, f32[8,128]{1,0:T(8,128)S(1)}, bf16[8,128,128]{2,1,0:T(8,128)(2,1)S(1...) custom-call(bf16[1,896,2048]{2,1,0:T(8,128)(2,1)} %w_ref.1, s32[1,896]{1,0:T(1,128)} %lb_ref.1, ...), custom_call_target="tpu_custom_call" | custom-call | tf_op jit(solution)/shard_map/rotate/pallas_call | solution.py:443
  87.5 2.2 %finish.1 = (bf16[1,896,2048]{2,1,0:T(8,128)(2,1)}, f32[1,896,256]{2,1,0:T(8,128)}, f32[1,16]{1,0:T(1,128)}, f32[1,1]{1,0:T(1,128)}, f32[1,1]{1,0:T(1,128)}) custom-call(bf16[1,896,2048]{2,1,0:T(8,128)(2,1)S(1)} %get-tuple-element.17.scaled, f32[1,896,256]{2,1,0:T(8,128)S(1)} %get-tuple-element.18.errors, f32[8,128]{1,0:T(8,128)S(1)} %get-tuple-element.19.small, ...), custom_call_target="tpu_custom_call" | custom-call | tf_op jit(solution)/shard_map/finish/pallas_call | solution.py:500

commit v5 on v4

--- a/solution.py
+++ b/solution.py
@@ -194,8 +194,9 @@
         return carry
 
     lax.fori_loop(1, MINE, column_step, 0)
-    for p in row_peer:
-        push(sb1.at[1, p], rb1.at[1, me], s1_send.at[1], s1_recv.at[1], {"row": p})
+    for i in range(MINE):
+        for p in row_peer:
+            push(sb1.at[1, p, i], rb1.at[1, me, i], s1_send.at[1], s1_recv.at[1], {"row": p})
     for n, (p, high) in enumerate(zip(ex_peer, higher)):
 
         @pl.when(high)

time: 89.8 us -> 89.9 us (level)
  no operation moved by 1% of the time
where the time goes in v5:
time: 89.9 us; the launch traced here: 89.8 us
  Pallas kernels  89.1 us (99%)
    pallas_call x1, Pallas kernels, body(): pl.pallas_call(rotate_kernel, out_shape=(pltpu.VMEM((1, rows, FF), BF16),...  86.9 us
    pallas_call x1, Pallas kernels, body(): pl.pallas_call(finish_kernel, out_shape=(jax.ShapeDtypeStruct((1, rows, F...  2.2 us

profile of v5, /device:TPU:0, one launch (start us, length us, event | category | flops | bytes accessed | tf_op | source)
XLA Modules:
  0.0 89.8 jit_solution(1796046525603186265)
XLA Ops:
  0.6 86.9 %rotate.1 = (bf16[1,896,2048]{2,1,0:T(8,128)(2,1)S(1)}, f32[1,896,256]{2,1,0:T(8,128)S(1)}, f32[8,128]{1,0:T(8,128)S(1)}, bf16[8,128,128]{2,1,0:T(8,128)(2,1)S(1...) custom-call(bf16[1,896,2048]{2,1,0:T(8,128)(2,1)} %w_ref.1, s32[1,896]{1,0:T(1,128)} %lb_ref.1, ...), custom_call_target="tpu_custom_call" | custom-call | tf_op jit(solution)/shard_map/rotate/pallas_call | solution.py:444
  87.6 2.2 %finish.1 = (bf16[1,896,2048]{2,1,0:T(8,128)(2,1)}, f32[1,896,256]{2,1,0:T(8,128)}, f32[1,16]{1,0:T(1,128)}, f32[1,1]{1,0:T(1,128)}, f32[1,1]{1,0:T(1,128)}) custom-call(bf16[1,896,2048]{2,1,0:T(8,128)(2,1)S(1)} %get-tuple-element.17.scaled, f32[1,896,256]{2,1,0:T(8,128)S(1)} %get-tuple-element.18.errors, f32[8,128]{1,0:T(8,128)S(1)} %get-tuple-element.19.small, ...), custom_call_target="tpu_custom_call" | custom-call | tf_op jit(solution)/shard_map/finish/pallas_call | solution.py:501
